TPU v7x, 32 devices: a whole 2x2x4 slice. The times are simulated.
32 devices in a mesh: dp: 8 (over y, x, core), tensor: 4 (over z).
Axes of the slice: x: 2, y: 2, z: 4, core: 2. Of those that a mesh axis runs over, the one named last changes fastest.
Arguments:
- tokens: bfloat16 [128, 5376], P('dp'), may hold values from -6 to 6
- lengths: int32 [128], P('dp'), may hold values from 1 to 1024, as said below
- positions: int32 [128], P('dp'), may hold values from 1 to 33791, as said below
- in_gain: float32 [5376], replicated, may hold values from 0.25 to 1.75
- q_weight: bfloat16 [5376, 4096], P('dp', 'tensor'), may hold values from -0.078125 to 0.078125
- k_weight: bfloat16 [5376, 2048], P('dp', 'tensor'), may hold values from -0.078125 to 0.078125
- v_weight: bfloat16 [5376, 2048], P('dp', 'tensor'), may hold values from -0.078125 to 0.078125
- q_gain: float32 [128], replicated, may hold values from 0.1 to 1.9
- k_gain: float32 [128], replicated, may hold values from 0.1 to 1.9
- key_cache: bfloat16 [128, 1024, 2048], P('dp', None, 'tensor'), may hold values from -480 to 480
- value_cache: bfloat16 [128, 1024, 2048], P('dp', None, 'tensor'), may hold values from -6 to 6
- out_weight: bfloat16 [4096, 5376], P('tensor', 'dp'), may hold values from -0.09375 to 0.09375
- post_gain: float32 [5376], replicated, may hold values from 0.25 to 1.75
Outputs:
- hidden_out: bfloat16 [128, 5376], P('dp')
- new_keys: bfloat16 [128, 2048], P('dp', 'tensor')
- new_values: bfloat16 [128, 2048], P('dp', 'tensor')
Inputs may be any that keep to these rules, and one draw needn't show every extreme that they name: Slots 0 to lengths - 1 of a sequence hold its cache; some sequence has exactly 1024. `positions`: each position is at least the sequence's length.
All inputs are finite; a program needn't handle non-finite values.
Results may differ from a plain program's by a relative error of at most 0.012.
The roundings to bfloat16 on the way count: a program that leaves them out, or rounds other values in their place, can miss the bound.
Values may be sent and summed in bfloat16 or wider, within the bound.
A program may use at most 64 MiB of HBM per device.

v0:
```python
import functools

import jax
import jax.numpy as jnp
import numpy as np
from jax import lax
from jax.experimental import pallas as pl
from jax.experimental.pallas import tpu as pltpu
from jax.sharding import PartitionSpec as P

HD = 128
QPRE = 168
LIMIT = 54000000
CHUNKS = 4
EARLY = 4
READY = 12

epsilon = 1e-06
rope_base = 1000000.0
rope_factor = 8.0

MESH = pl.DeviceIdType.MESH
VMEM = pltpu.VMEM
SMEM = pltpu.SMEM
F32 = jnp.float32
BF16 = jnp.bfloat16


def flip(a, b, n):
    total, bit = 0, 1
    while bit < n:
        total = total + lax.rem(a // bit + b // bit, 2) * bit
        bit *= 2
    return total


def layer_kernel(
    n, m, tok_hbm, len_hbm, pos_hbm, freq_hbm, gain_hbm, wq_hbm, wk_hbm, wv_hbm, qg_hbm, kg_hbm,
    kc_hbm, vc_hbm, wo_hbm, post_hbm,
    hid_out, nk_out, nv_out,
    tok_v, len_s, pos_s, tables, gains, w, kbuf, vbuf, turned, wo, wt,
    sbuf, rbuf, keep, pout, pin, rs, rr, q_s, kx_s, vx_s, scores, weights, sums, owns, mixed,
    att, gath, ps, pr, fs, fr,
    lsem, wsem, ksem, vsem, osem, s1, r1, sp, rp, s2, r2, s3, r3, s4, r4, s5, r5,
):
    me = lax.axis_index("dp")
    mt = lax.axis_index("tensor")
    rows, width = tok_v.shape
    depth, cols = w.shape
    qc, kc = wq_hbm.shape[1], wk_hbm.shape[1]
    ctx = kbuf.shape[1]
    ocols = wo.shape[0]
    heads, groups = qc // HD, kc // HD
    per = heads // groups
    half = n // 2
    part = rows // CHUNKS
    ready = turned.shape[0]
    chunk = min(512, cols)
    chunks = cols // chunk

    barrier = pltpu.get_barrier_semaphore()
    for a in range(1, n):
        pl.semaphore_signal(
            barrier, inc=1, device_id={"dp": lax.rem(me + a, n), "tensor": mt}, device_id_type=MESH)
    for b in range(1, m):
        pl.semaphore_signal(
            barrier, inc=1, device_id={"dp": me, "tensor": lax.rem(mt + b, m)}, device_id_type=MESH)

    copy = pltpu.make_async_copy
    small = [
        copy(tok_hbm, tok_v, lsem.at[0]),
        copy(gain_hbm, gains.at[0], lsem.at[1]),
        copy(post_hbm, gains.at[1], lsem.at[1]),
        copy(qg_hbm, tables.at[0], lsem.at[2]),
        copy(kg_hbm, tables.at[1], lsem.at[2]),
        copy(freq_hbm, tables.at[2], lsem.at[2]),
        copy(len_hbm, len_s, lsem.at[3]),
        copy(pos_hbm, pos_s, lsem.at[4]),
    ]
    loads = [
        copy(wq_hbm, w.at[:, pl.ds(0, qc)], wsem.at[0]),
        copy(wk_hbm, w.at[:, pl.ds(qc, kc)], wsem.at[1]),
        copy(wv_hbm, w.at[:, pl.ds(qc + kc, kc)], wsem.at[1]),
    ]
    keys = [copy(kc_hbm.at[b], kbuf.at[b % ready], ksem.at[b // 2]) for b in range(rows)]
    values = [copy(vc_hbm.at[b], vbuf.at[b], vsem.at[b // 2]) for b in range(rows)]

    def settle(ref, sem):
        copy(ref, ref, sem).wait()

    wload = copy(wo_hbm, wo, osem)
    for load in small + loads + [wload]:
        load.start()

    with jax.named_scope("norm"):
        with jax.named_scope("tokwait"):
            settle(tok_v, lsem.at[0])
        settle(gains, lsem.at[1])
        for load in keys[:EARLY]:
            load.start()
        tok = tok_v[...].astype(F32)
        scale = lax.rsqrt(jnp.sum(tok * tok, axis=-1, keepdims=True) * (1.0 / width) + epsilon)
        normed = jnp.concatenate([
            (tok[:, k * HD : (k + 1) * HD] * scale * gains[0, k : k + 1, :]).astype(BF16)
            for k in range(width // HD)
        ], axis=1)
        for d in range(n):
            sbuf[d] = normed[:, d * depth : (d + 1) * depth]
    with jax.named_scope("barrier"):
        pl.semaphore_wait(barrier, n + m - 2)

    def turn(first, last):
        for b in range(first, last, 2):
            settle(kbuf.at[pl.ds(b, 2)], ksem.at[b // 2])

        @pl.loop(first, last)
        def _(b):
            turned[b] = kbuf[b].T

    def spread(j):
        to = flip(me, j, n)
        return pltpu.make_async_remote_copy(
            src_ref=sbuf.at[to], dst_ref=rbuf.at[j], send_sem=s1, recv_sem=r1,
            device_id={"dp": to, "tensor": mt}, device_id_type=MESH)

    with jax.named_scope("spread"):
        for j in range(n - 1, 0, -1):
            spread(j).start()
        rbuf[0] = sbuf[me]

    with jax.named_scope("loadwait"):
        settle(tables, lsem.at[2])
        small[6].wait()
        small[7].wait()
        settle(w.at[:, pl.ds(0, qc)], wsem.at[0])
        settle(w.at[:, pl.ds(qc, 2 * kc)], wsem.at[1])
        wload.wait()
        for load in keys[EARLY:ready]:
            load.start()
    with jax.named_scope("rope"):
        row = lax.broadcasted_iota(jnp.int32, (rows, HD), 0)
        lane = lax.broadcasted_iota(jnp.int32, (rows, HD), 1)
        position = jnp.zeros((rows, HD), jnp.int32)
        for r in range(rows):
            position = jnp.where(row == r, pos_s[r], position)
        angles = position.astype(F32) / rope_factor * tables[2]
        cos_part = jnp.cos(angles)
        sin_part = jnp.sin(angles)
        sin_part = jnp.where(lane < HD // 2, -sin_part, sin_part)

    with jax.named_scope("turn"):
        wt[...] = wo[...].T
        turn(0, EARLY)
        for load in keys[ready:]:
            load.start()
    with jax.named_scope("spreadwait"):
        settle(rbuf.at[pl.ds(1, n - 1)], r1)
    for load in values:
        load.start()
    x = rbuf[...].reshape(n * rows, depth)

    def pair(c):
        span = pl.ds(c * chunk, chunk)
        return pltpu.make_async_remote_copy(
            src_ref=pout.at[:, :, span], dst_ref=pin.at[:, :, span], send_sem=sp, recv_sem=rp.at[c],
            device_id={"dp": flip(me, 1, n), "tensor": mt}, device_id_type=MESH)

    def give(i, c):
        span = pl.ds(c * chunk, chunk)
        return pltpu.make_async_remote_copy(
            src_ref=rs.at[i, :, span], dst_ref=rr.at[i, :, span], send_sem=s2, recv_sem=r2.at[c],
            device_id={"dp": flip(me, 2 * i, n), "tensor": mt}, device_id_type=MESH)

    with jax.named_scope("mm"):
        for c in range(chunks):
            at = slice(c * chunk, (c + 1) * chunk)
            product = jnp.dot(x, w[:, at], preferred_element_type=F32).reshape(n, rows, chunk)
            for i in range(half):
                pout[i, :, at] = product[2 * i + 1].astype(BF16)
            pair(c).start()
            for i in range(half):
                keep[i, :, at] = product[2 * i]
    with jax.named_scope("pair"):
        for c in range(chunks):
            at = slice(c * chunk, (c + 1) * chunk)
            pair(c).wait_recv()
            for i in range(half - 1, 0, -1):
                rs[i, :, at] = (keep[i, :, at] + pin[i, :, at].astype(F32)).astype(BF16)
                give(i, c).start()

    with jax.named_scope("turnkeys"):
        turn(EARLY, ready)

    def head(block, gain):
        mean = jnp.mean(block * block, axis=-1, keepdims=True)
        block = block * lax.rsqrt(mean + epsilon) * gain
        return block * cos_part + pltpu.roll(block, HD // 2, 1) * sin_part

    for c in range(chunks):
        at = slice(c * chunk, (c + 1) * chunk)
        with jax.named_scope("givewait"):
            settle(rr.at[pl.ds(1, half - 1), :, pl.ds(c * chunk, chunk)], r2.at[c])
        total = keep[0, :, at] + pin[0, :, at].astype(F32)
        for i in range(1, half):
            total = total + rr[i, :, at].astype(F32)
        for k in range(chunk // HD):
            block = total[:, k * HD : (k + 1) * HD]
            h = (c * chunk) // HD + k
            if h < heads:
                query = head(block, tables[0]) * QPRE ** (-0.5)
                q_s[:, h, :] = query.astype(BF16).astype(F32)
            elif h < heads + groups:
                g = h - heads
                key = head(block, tables[1]).astype(BF16)
                nk_out[:, g * HD : (g + 1) * HD] = key
                for r in range(per):
                    kx_s[:, g * per + r, :] = key.astype(F32)
            else:
                g = h - heads - groups
                value = block.astype(BF16)
                nv_out[:, g * HD : (g + 1) * HD] = value
                for r in range(per):
                    vx_s[:, g * per + r, :] = value.astype(F32)

    def gather(c, j):
        return pltpu.make_async_remote_copy(
            src_ref=att.at[c], dst_ref=gath.at[c, j], send_sem=s3, recv_sem=r3.at[c],
            device_id={"dp": flip(me, j, n), "tensor": mt}, device_id_type=MESH)

    middle = (m // 2 - 1, m // 2)
    quarter = n // 4
    slots = (
        [*range(quarter), *range(n - quarter, n)],
        [*range(quarter, n - quarter)],
    )

    def reduce(c, h):
        return pltpu.make_async_remote_copy(
            src_ref=ps.at[c, h], dst_ref=pr.at[c, mt], send_sem=s4, recv_sem=r4.at[c],
            device_id={"dp": me, "tensor": middle[h]}, device_id_type=MESH)

    def final(c, i, j, b):
        return pltpu.make_async_remote_copy(
            src_ref=fs.at[c, i], dst_ref=fr.at[c, me], send_sem=s5.at[b], recv_sem=r5.at[c],
            device_id={"dp": flip(me, j, n), "tensor": b}, device_id_type=MESH)

    which = lax.broadcasted_iota(jnp.int32, (heads, HD), 0) // per
    slot = lax.broadcasted_iota(jnp.int32, (heads, ctx), 1)

    def score(c):
        for b in range(c * part, (c + 1) * part):
            q8 = q_s[b]
            wide = jnp.concatenate(
                [jnp.where(which == g, q8, 0.0) for g in range(groups)], axis=1).astype(BF16)
            if b < ready:
                scores[b] = jnp.dot(wide, turned[b], preferred_element_type=F32)
            else:
                scores[b] = lax.dot_general(
                    wide, kbuf[b - ready], (((1,), (1,)), ((), ())), preferred_element_type=F32)

    def mix(c):
        for b in range(c * part, (c + 1) * part):
            own = jnp.sum(q_s[b] * kx_s[b], axis=-1, keepdims=True)
            s = jnp.where(slot < len_s[b], scores[b], -jnp.inf)
            largest = jnp.maximum(jnp.max(s, axis=-1, keepdims=True), own)
            e = jnp.exp(s - largest)
            e_own = jnp.exp(own - largest)
            sums[b] = jnp.broadcast_to(jnp.sum(e, axis=-1, keepdims=True) + e_own, (heads, HD))
            owns[b] = e_own.astype(BF16).astype(F32) * vx_s[b]
            weights[b] = e.astype(BF16)
        for b in range(c * part, (c + 1) * part):
            mixture = jnp.dot(weights[b], vbuf[b], preferred_element_type=F32)
            got = mixture[:, :HD]
            for g in range(1, groups):
                got = jnp.where(which == g, mixture[:, g * HD : (g + 1) * HD], got)
            mixed[b] = (got + owns[b]) / sums[b]
        for h in range(heads):
            att[c, :, h * HD : (h + 1) * HD] = mixed[c * part : (c + 1) * part, h, :].astype(BF16)
        for j in range(n - 1, 0, -1):
            gather(c, j).start()
        gath[c, 0] = att[c]

    def project(c):
        with jax.named_scope("gatherwait"):
            settle(gath.at[c, pl.ds(1, n - 1)], r3.at[c])
        y = lax.dot_general(
            gath[c].reshape(n * part, qc), wt[...], (((1,), (0,)), ((), ())), preferred_element_type=F32)
        y = y.astype(BF16)
        edge = quarter * part
        ps[c, 0, :edge] = y[:edge]
        ps[c, 0, edge:] = y[3 * edge :]
        ps[c, 1] = y[edge : 3 * edge]
        for h in range(2):
            @pl.when(mt != middle[h])
            def _():
                reduce(c, h).start()

    def total(c):
        for h in range(2):
            @pl.when(mt == middle[h])
            def _():
                pr[c, middle[h]] = ps[c, h]
                with jax.named_scope("reducewait"):
                    settle(pr.at[c, pl.ds(1, m - 1)], r4.at[c])
                got = pr[c, 0].astype(F32)
                for t in range(1, m):
                    got = got + pr[c, t].astype(F32)
                for i, j in enumerate(slots[h]):
                    fs[c, i] = got[i * part : (i + 1) * part].astype(BF16)
                far = sorted(range(m), key=lambda b: -abs(b - middle[h]))
                for b in far:
                    for i, j in reversed([*enumerate(slots[h])]):
                        if (j, b) == (0, middle[0]):
                            fr[c, me] = fs[c, i]
                        else:
                            final(c, i, j, b).start()

    def finish(c):
        with jax.named_scope("finalwait"):
            @pl.when(mt == middle[0])
            def _():
                settle(fr.at[c, pl.ds(0, n - 1)], r5.at[c])

            @pl.when(mt != middle[0])
            def _():
                settle(fr.at[c], r5.at[c])

        blocks = [fr[c, d].astype(F32) for d in range(n)]
        square = jnp.zeros((part, 1), F32)
        for block in blocks:
            square = square + jnp.sum(block * block, axis=-1, keepdims=True)
        factor = lax.rsqrt(square * (1.0 / width) + epsilon)
        y = jnp.concatenate(blocks, axis=1)
        mine = slice(c * part, (c + 1) * part)
        for k in range(width // HD):
            at = slice(k * HD, (k + 1) * HD)
            hid_out[mine, at] = (
                tok_v[mine, at].astype(F32) + y[:, at] * factor * gains[1, k : k + 1, :]).astype(BF16)

    def run(step, c):
        with jax.named_scope(step.__name__):
            step(c)

    with jax.named_scope("cachewait"):
        for b in range(ready, rows, 2):
            settle(kbuf.at[pl.ds(b - ready, 2)], ksem.at[b // 2])
        for b in range(0, rows, 2):
            settle(vbuf.at[pl.ds(b, 2)], vsem.at[b // 2])
    run(score, 0)
    for c in range(CHUNKS):
        if c + 1 < CHUNKS:
            run(score, c + 1)
        else:
            run(project, 0)
        run(mix, c)
    for c in range(1, CHUNKS):
        run(project, c)
    for c in range(CHUNKS):
        run(total, c)
    for c in range(CHUNKS):
        run(finish, c)

    with jax.named_scope("drain"):
        settle(rbuf.at[pl.ds(1, n - 1)], s1)
        settle(pout, sp)
        settle(rs.at[pl.ds(1, half - 1)], s2)
        settle(gath.at[:, pl.ds(1, n - 1)], s3)

        for h in range(2):
            @pl.when(mt == middle[h])
            def _():
                settle(ps.at[:, 0], s4)
                for b in range(m):
                    count = half - 1 if (h, b) == (0, middle[0]) else half
                    settle(fr.at[:, pl.ds(0, count)], s5.at[b])

        @pl.when((mt < middle[0]) | (mt > middle[1]))
        def _():
            settle(ps, s4)


def store_kernel(hid_v, nk_v, nv_v, hid_out, nk_out, nv_out, sem):
    copies = [
        pltpu.make_async_copy(hid_v, hid_out, sem.at[0]),
        pltpu.make_async_copy(nk_v, nk_out, sem.at[1]),
        pltpu.make_async_copy(nv_v, nv_out, sem.at[2]),
    ]
    for move in copies:
        move.start()
    for move in copies:
        move.wait()


def per_device(
    n, m, tokens, lengths, positions, in_gain, q_weight, k_weight, v_weight, q_gain, k_gain,
    key_cache, value_cache, out_weight, post_gain,
):
    rows, width = tokens.shape
    depth, qc = q_weight.shape
    kc = k_weight.shape[1]
    cols = qc + 2 * kc
    chunks = cols // min(512, cols)
    heads = qc // HD
    ctx = key_cache.shape[1]
    ocols = out_weight.shape[1]
    part = rows // CHUNKS
    half = n // 2
    exponent = np.arange(HD // 2) * (2.0 / HD)
    frequency = np.power(rope_base, -exponent).astype(np.float32)
    frequency = np.concatenate([frequency, frequency])[None, :]

    full = pl.BlockSpec(memory_space=VMEM)
    anywhere = pl.BlockSpec(memory_space=pltpu.HBM)
    dma = pltpu.SemaphoreType.DMA
    results = [
        jax.ShapeDtypeStruct((rows, width), BF16),
        jax.ShapeDtypeStruct((rows, kc), BF16),
        jax.ShapeDtypeStruct((rows, kc), BF16),
    ]
    made = pl.pallas_call(
        functools.partial(layer_kernel, n, m),
        name="layer",
        out_shape=results,
        in_specs=[anywhere] * 14,
        out_specs=[full] * 3,
        scratch_shapes=[
            VMEM((rows, width), BF16),
            SMEM((rows,), jnp.int32),
            SMEM((rows,), jnp.int32),
            VMEM((3, 1, HD), F32),
            VMEM((2, width // HD, HD), F32),
            VMEM((depth, cols), BF16),
            VMEM((READY, ctx, kc), BF16),
            VMEM((rows, ctx, kc), BF16),
            VMEM((READY, kc, ctx), BF16),
            VMEM((ocols, qc), BF16),
            VMEM((qc, ocols), BF16),
            VMEM((n, rows, depth), BF16),
            VMEM((n, rows, depth), BF16),
            VMEM((half, rows, cols), F32),
            VMEM((half, rows, cols), BF16),
            VMEM((half, rows, cols), BF16),
            VMEM((half, rows, cols), BF16),
            VMEM((half, rows, cols), BF16),
            VMEM((rows, heads, HD), F32),
            VMEM((rows, heads, HD), F32),
            VMEM((rows, heads, HD), F32),
            VMEM((rows, heads, ctx), F32),
            VMEM((rows, heads, ctx), BF16),
            VMEM((rows, heads, HD), F32),
            VMEM((rows, heads, HD), F32),
            VMEM((rows, heads, HD), F32),
            VMEM((CHUNKS, part, qc), BF16),
            VMEM((CHUNKS, n, part, qc), BF16),
            VMEM((CHUNKS, 2, half * part, ocols), BF16),
            VMEM((CHUNKS, m, half * part, ocols), BF16),
            VMEM((CHUNKS, half, part, ocols), BF16),
            VMEM((CHUNKS, n, part, ocols), BF16),
            dma((5,)), dma((2,)), dma((rows // 2,)), dma((rows // 2,)), dma, dma, dma, dma, dma((chunks,)), dma, dma((chunks,)),
            dma, dma((CHUNKS,)), dma, dma((CHUNKS,)), dma((m,)), dma((CHUNKS,)),
        ],
        compiler_params=pltpu.CompilerParams(
            collective_id=0, has_side_effects=True, vmem_limit_bytes=LIMIT),
    )(*[pltpu.with_memory_space_constraint(operand, pltpu.HBM) for operand in (
        tokens, lengths, positions, jnp.asarray(frequency), in_gain.reshape(width // HD, HD),
        q_weight, k_weight, v_weight, q_gain[None, :], k_gain[None, :],
        key_cache, value_cache, out_weight.T, post_gain.reshape(width // HD, HD))])
    return pl.pallas_call(
        store_kernel,
        name="store",
        out_shape=results,
        in_specs=[full] * 3,
        out_specs=[anywhere] * 3,
        scratch_shapes=[dma((3,))],
        compiler_params=pltpu.CompilerParams(vmem_limit_bytes=1 << 20),
    )(*made)


def solution(mesh):
    n, m = mesh.shape["dp"], mesh.shape["tensor"]
    return jax.shard_map(
        functools.partial(per_device, n, m),
        mesh=mesh,
        in_specs=(
            P("dp", None),
            P("dp"),
            P("dp"),
            P(),
            P("dp", "tensor"),
            P("dp", "tensor"),
            P("dp", "tensor"),
            P(),
            P(),
            P("dp", None, "tensor"),
            P("dp", None, "tensor"),
            P("tensor", "dp"),
            P(),
        ),
        out_specs=(P("dp", None), P("dp", "tensor"), P("dp", "tensor")),
        check_vma=False,
    )
```

profile of v0, /device:TPU:0, one launch (start us, length us, event | category | flops | bytes accessed | tf_op | source)
XLA Modules:
  0.0 35.4 jit_solution(1756306315706623644)
XLA Ops:
  0.6 34.1 %layer.1 = (bf16[16,5376]{1,0:T(8,128)(2,1)S(1)}, bf16[16,512]{1,0:T(8,128)(2,1)S(1)}, bf16[16,512]{1,0:T(8,128)(2,1)S(1)}) custom-call(bf16[16,5376]{1,0:T(8,128)(2,1)} %tok_hbm.1, s32[16]{0:T(128)} %len_hbm.1, s32[16]{0:T(128)} %pos_hbm.1, f32[1,128]{1,0:T(1,128)} %constant.2.clone.freq_hbm, f32[42,128]{1,0:T(8,128)} %bitcast.6, bf16[672,1024]{1,0:T(8,128)(2,1)} %wq_hbm.1, ...), custom_call_target="tpu_custom_call" | custom-call | tf_op jit(solution)/shard_map/layer/pallas_call | solution.py:420
  34.7 0.7 %store.1 = (bf16[16,5376]{1,0:T(8,128)(2,1)}, bf16[16,512]{1,0:T(8,128)(2,1)}, bf16[16,512]{1,0:T(8,128)(2,1)}) custom-call(bf16[16,5376]{1,0:T(8,128)(2,1)S(1)} %get-tuple-element.6.hid_v, bf16[16,512]{1,0:T(8,128)(2,1)S(1)} %get-tuple-element.7.nk_v, bf16[16,512]{1,0:T(8,128)(2,1)S(1)} %get-tuple-element.8.nv_v), custom_call_target="tpu_custom_call" | custom-call | tf_op jit(solution)/shard_map/store/pallas_call | solution.py:468
where the time goes:
time: 35.6 us; the launch traced here: 35.4 us
  Pallas kernels  34.8 us (98%)
  between operations  0.64 us (2%)
    pallas_call x1, Pallas kernels, per_device(): pl.pallas_call(functools.partial(layer_kernel, n, m), name='layer', out_s...  34.1 us

commit v1 on v0

--- a/solution.py
+++ b/solution.py
@@ -82,8 +82,8 @@
         copy(wk_hbm, w.at[:, pl.ds(qc, kc)], wsem.at[1]),
         copy(wv_hbm, w.at[:, pl.ds(qc + kc, kc)], wsem.at[1]),
     ]
-    keys = [copy(kc_hbm.at[b], kbuf.at[b % ready], ksem.at[b // 2]) for b in range(rows)]
-    values = [copy(vc_hbm.at[b], vbuf.at[b], vsem.at[b // 2]) for b in range(rows)]
+    keys = [copy(kc_hbm.at[b], kbuf.at[b % ready], ksem.at[b // part]) for b in range(rows)]
+    values = [copy(vc_hbm.at[b], vbuf.at[b], vsem.at[b // part]) for b in range(rows)]
 
     def settle(ref, sem):
         copy(ref, ref, sem).wait()
@@ -110,8 +110,8 @@
         pl.semaphore_wait(barrier, n + m - 2)
 
     def turn(first, last):
-        for b in range(first, last, 2):
-            settle(kbuf.at[pl.ds(b, 2)], ksem.at[b // 2])
+        for b in range(first, last, part):
+            settle(kbuf.at[pl.ds(b, part)], ksem.at[b // part])
 
         @pl.loop(first, last)
         def _(b):
@@ -196,7 +196,7 @@
         block = block * lax.rsqrt(mean + epsilon) * gain
         return block * cos_part + pltpu.roll(block, HD // 2, 1) * sin_part
 
-    for c in range(chunks):
+    def split(c):
         at = slice(c * chunk, (c + 1) * chunk)
         with jax.named_scope("givewait"):
             settle(rr.at[pl.ds(1, half - 1), :, pl.ds(c * chunk, chunk)], r2.at[c])
@@ -247,18 +247,23 @@
     which = lax.broadcasted_iota(jnp.int32, (heads, HD), 0) // per
     slot = lax.broadcasted_iota(jnp.int32, (heads, ctx), 1)
 
-    def score(c):
+    some = chunk // HD
+    wide = some // per * HD
+
+    def score(c, p):
         for b in range(c * part, (c + 1) * part):
-            q8 = q_s[b]
-            wide = jnp.concatenate(
-                [jnp.where(which == g, q8, 0.0) for g in range(groups)], axis=1).astype(BF16)
+            q = q_s[b, p * some : (p + 1) * some, :]
+            q = jnp.concatenate(
+                [jnp.where(which[:some] == g, q, 0.0) for g in range(some // per)], axis=1).astype(BF16)
+            at = slice(p * wide, (p + 1) * wide)
             if b < ready:
-                scores[b] = jnp.dot(wide, turned[b], preferred_element_type=F32)
+                got = jnp.dot(q, turned[b, at, :], preferred_element_type=F32)
             else:
-                scores[b] = lax.dot_general(
-                    wide, kbuf[b - ready], (((1,), (1,)), ((), ())), preferred_element_type=F32)
-
-    def mix(c):
+                got = lax.dot_general(
+                    q, kbuf[b - ready, :, at], (((1,), (1,)), ((), ())), preferred_element_type=F32)
+            scores[b, p * some : (p + 1) * some, :] = got
+
+    def soft(c):
         for b in range(c * part, (c + 1) * part):
             own = jnp.sum(q_s[b] * kx_s[b], axis=-1, keepdims=True)
             s = jnp.where(slot < len_s[b], scores[b], -jnp.inf)
@@ -268,6 +273,8 @@
             sums[b] = jnp.broadcast_to(jnp.sum(e, axis=-1, keepdims=True) + e_own, (heads, HD))
             owns[b] = e_own.astype(BF16).astype(F32) * vx_s[b]
             weights[b] = e.astype(BF16)
+
+    def mix(c):
         for b in range(c * part, (c + 1) * part):
             mixture = jnp.dot(weights[b], vbuf[b], preferred_element_type=F32)
             got = mixture[:, :HD]
@@ -337,22 +344,30 @@
             hid_out[mine, at] = (
                 tok_v[mine, at].astype(F32) + y[:, at] * factor * gains[1, k : k + 1, :]).astype(BF16)
 
-    def run(step, c):
+    def run(step, *which):
         with jax.named_scope(step.__name__):
-            step(c)
-
+            step(*which)
+
+    lead = qc // chunk
     with jax.named_scope("cachewait"):
-        for b in range(ready, rows, 2):
-            settle(kbuf.at[pl.ds(b - ready, 2)], ksem.at[b // 2])
-        for b in range(0, rows, 2):
-            settle(vbuf.at[pl.ds(b, 2)], vsem.at[b // 2])
-    run(score, 0)
+        for b in range(ready, rows, part):
+            settle(kbuf.at[pl.ds(b - ready, part)], ksem.at[b // part])
+    for p in range(lead):
+        run(split, p)
+        for c in range(2):
+            run(score, c, p)
+    for c in range(lead, chunks):
+        run(split, c)
+    with jax.named_scope("valueswait"):
+        for b in range(0, rows, part):
+            settle(vbuf.at[pl.ds(b, part)], vsem.at[b // part])
     for c in range(CHUNKS):
-        if c + 1 < CHUNKS:
-            run(score, c + 1)
-        else:
-            run(project, 0)
+        if 0 < c < CHUNKS - 1:
+            for p in range(lead):
+                run(score, c + 1, p)
+        run(soft, c)
         run(mix, c)
+    run(project, 0)
     for c in range(1, CHUNKS):
         run(project, c)
     for c in range(CHUNKS):
@@ -456,7 +471,7 @@
             VMEM((CHUNKS, m, half * part, ocols), BF16),
             VMEM((CHUNKS, half, part, ocols), BF16),
             VMEM((CHUNKS, n, part, ocols), BF16),
-            dma((5,)), dma((2,)), dma((rows // 2,)), dma((rows // 2,)), dma, dma, dma, dma, dma((chunks,)), dma, dma((chunks,)),
+            dma((5,)), dma((2,)), dma((CHUNKS,)), dma((CHUNKS,)), dma, dma, dma, dma, dma((chunks,)), dma, dma((chunks,)),
             dma, dma((CHUNKS,)), dma, dma((CHUNKS,)), dma((m,)), dma((CHUNKS,)),
         ],
         compiler_params=pltpu.CompilerParams(

time: 35.6 us -> 34.6 us (0.972)
  Pallas kernels: 34.8 us -> 33.8 us
    pallas_call x1, Pallas kernels: 34.1 us -> 33.1 us  [per_device(): pl.pallas_call(functools.partial(layer_kernel, n, m), name='layer', out_s...]
where the time goes in v1:
time: 34.6 us; the launch traced here: 34.5 us
  Pallas kernels  33.8 us (98%)
  between operations  0.64 us (2%)
    pallas_call x1, Pallas kernels, per_device(): pl.pallas_call(functools.partial(layer_kernel, n, m), name='layer', out_s...  33.1 us
    pallas_call x1, Pallas kernels, per_device(): pl.pallas_call(store_kernel, name='store', out_shape=results, in_specs=[f...  0.7 us

profile of v1, /device:TPU:0, one launch (start us, length us, event | category | flops | bytes accessed | tf_op | source)
XLA Modules:
  0.0 34.5 jit_solution(1543091663421363153)
XLA Ops:
  0.6 33.1 %layer.1 = (bf16[16,5376]{1,0:T(8,128)(2,1)S(1)}, bf16[16,512]{1,0:T(8,128)(2,1)S(1)}, bf16[16,512]{1,0:T(8,128)(2,1)S(1)}) custom-call(bf16[16,5376]{1,0:T(8,128)(2,1)} %tok_hbm.1, s32[16]{0:T(128)} %len_hbm.1, s32[16]{0:T(128)} %pos_hbm.1, f32[1,128]{1,0:T(1,128)} %constant.2.clone.freq_hbm, f32[42,128]{1,0:T(8,128)} %bitcast.6, bf16[672,1024]{1,0:T(8,128)(2,1)} %wq_hbm.1, ...), custom_call_target="tpu_custom_call" | custom-call | tf_op jit(solution)/shard_map/layer/pallas_call | solution.py:435
  33.8 0.7 %store.1 = (bf16[16,5376]{1,0:T(8,128)(2,1)}, bf16[16,512]{1,0:T(8,128)(2,1)}, bf16[16,512]{1,0:T(8,128)(2,1)}) custom-call(bf16[16,5376]{1,0:T(8,128)(2,1)S(1)} %get-tuple-element.6.hid_v, bf16[16,512]{1,0:T(8,128)(2,1)S(1)} %get-tuple-element.7.nk_v, bf16[16,512]{1,0:T(8,128)(2,1)S(1)} %get-tuple-element.8.nv_v), custom_call_target="tpu_custom_call" | custom-call | tf_op jit(solution)/shard_map/store/pallas_call | solution.py:483

commit v2 on v1

--- a/solution.py
+++ b/solution.py
@@ -213,14 +213,12 @@
                 g = h - heads
                 key = head(block, tables[1]).astype(BF16)
                 nk_out[:, g * HD : (g + 1) * HD] = key
-                for r in range(per):
-                    kx_s[:, g * per + r, :] = key.astype(F32)
+                kx_s[:, g, :] = key.astype(F32)
             else:
                 g = h - heads - groups
                 value = block.astype(BF16)
                 nv_out[:, g * HD : (g + 1) * HD] = value
-                for r in range(per):
-                    vx_s[:, g * per + r, :] = value.astype(F32)
+                vx_s[:, g, :] = value.astype(F32)
 
     def gather(c, j):
         return pltpu.make_async_remote_copy(
@@ -265,13 +263,14 @@
 
     def soft(c):
         for b in range(c * part, (c + 1) * part):
-            own = jnp.sum(q_s[b] * kx_s[b], axis=-1, keepdims=True)
+            new_key = jnp.repeat(kx_s[b], per, axis=0)
+            own = jnp.sum(q_s[b] * new_key, axis=-1, keepdims=True)
             s = jnp.where(slot < len_s[b], scores[b], -jnp.inf)
             largest = jnp.maximum(jnp.max(s, axis=-1, keepdims=True), own)
             e = jnp.exp(s - largest)
             e_own = jnp.exp(own - largest)
             sums[b] = jnp.broadcast_to(jnp.sum(e, axis=-1, keepdims=True) + e_own, (heads, HD))
-            owns[b] = e_own.astype(BF16).astype(F32) * vx_s[b]
+            owns[b] = e_own.astype(BF16).astype(F32) * jnp.repeat(vx_s[b], per, axis=0)
             weights[b] = e.astype(BF16)
 
     def mix(c):
@@ -297,10 +296,17 @@
         ps[c, 0, :edge] = y[:edge]
         ps[c, 0, edge:] = y[3 * edge :]
         ps[c, 1] = y[edge : 3 * edge]
-        for h in range(2):
-            @pl.when(mt != middle[h])
-            def _():
-                reduce(c, h).start()
+        @pl.when(mt <= middle[0])
+        def _():
+            reduce(c, 1).start()
+
+        @pl.when((mt < middle[0]) | (mt > middle[0]))
+        def _():
+            reduce(c, 0).start()
+
+        @pl.when(mt > middle[1])
+        def _():
+            reduce(c, 1).start()
 
     def total(c):
         for h in range(2):
@@ -458,8 +464,8 @@
             VMEM((half, rows, cols), BF16),
             VMEM((half, rows, cols), BF16),
             VMEM((rows, heads, HD), F32),
-            VMEM((rows, heads, HD), F32),
-            VMEM((rows, heads, HD), F32),
+            VMEM((rows, kc // HD, HD), F32),
+            VMEM((rows, kc // HD, HD), F32),
             VMEM((rows, heads, ctx), F32),
             VMEM((rows, heads, ctx), BF16),
             VMEM((rows, heads, HD), F32),

time: 34.6 us -> 34.6 us (level)
  no operation moved by 1% of the time
where the time goes in v2:
time: 34.6 us; the launch traced here: 34.4 us
  Pallas kernels  33.8 us (98%)
  between operations  0.64 us (2%)
    pallas_call x1, Pallas kernels, per_device(): pl.pallas_call(functools.partial(layer_kernel, n, m), name='layer', out_s...  33.1 us
    pallas_call x1, Pallas kernels, per_device(): pl.pallas_call(store_kernel, name='store', out_shape=results, in_specs=[f...  0.7 us

profile of v2, /device:TPU:0, one launch (start us, length us, event | category | flops | bytes accessed | tf_op | source)
XLA Modules:
  0.0 34.4 jit_solution(596994817314242117)
XLA Ops:
  0.6 33.1 %layer.1 = (bf16[16,5376]{1,0:T(8,128)(2,1)S(1)}, bf16[16,512]{1,0:T(8,128)(2,1)S(1)}, bf16[16,512]{1,0:T(8,128)(2,1)S(1)}) custom-call(bf16[16,5376]{1,0:T(8,128)(2,1)} %tok_hbm.1, s32[16]{0:T(128)} %len_hbm.1, s32[16]{0:T(128)} %pos_hbm.1, f32[1,128]{1,0:T(1,128)} %constant.2.clone.freq_hbm, f32[42,128]{1,0:T(8,128)} %bitcast.6, bf16[672,1024]{1,0:T(8,128)(2,1)} %wq_hbm.1, ...), custom_call_target="tpu_custom_call" | custom-call | tf_op jit(solution)/shard_map/layer/pallas_call | solution.py:441
  33.7 0.7 %store.1 = (bf16[16,5376]{1,0:T(8,128)(2,1)}, bf16[16,512]{1,0:T(8,128)(2,1)}, bf16[16,512]{1,0:T(8,128)(2,1)}) custom-call(bf16[16,5376]{1,0:T(8,128)(2,1)S(1)} %get-tuple-element.6.hid_v, bf16[16,512]{1,0:T(8,128)(2,1)S(1)} %get-tuple-element.7.nk_v, bf16[16,512]{1,0:T(8,128)(2,1)S(1)} %get-tuple-element.8.nv_v), custom_call_target="tpu_custom_call" | custom-call | tf_op jit(solution)/shard_map/store/pallas_call | solution.py:489
